TPU v7x, 32 devices: a whole 2x2x4 slice. The times are simulated.
32 devices in a mesh: blk: 16 (over z, y, core), head: 2 (over x).
Axes of the slice: x: 2, y: 2, z: 4, core: 2. Of those that a mesh axis runs over, the one named last changes fastest.
Arguments:
- queries: bfloat16 [8192, 16, 128], P('blk', 'head'), may hold values from -6 to 6
- out_grad: bfloat16 [8192, 16, 128], P('blk', 'head'), may hold values from -6 to 6
- outputs: bfloat16 [8192, 16, 128], P('blk', 'head'), may hold values from -6 to 6
- key_vectors: bfloat16 [8192, 128], P('blk'), may hold values from -6 to 6
- value_vectors: bfloat16 [8192, 128], P('blk'), may hold values from -6 to 6
- logsumexp: float32 [8192, 16], P('blk', 'head'), may hold values from 4 to 7
- positions: int32 [8192], P('blk'), may hold values from 0 to 8191, as said below
- doc_start: int32 [8192], P('blk'), may hold values from 0 to 8191, as said below
Outputs:
- query_grad: bfloat16 [8192, 16, 128], P('blk', 'head')
- key_grad: bfloat16 [8192, 128], P('blk')
- value_grad: bfloat16 [8192, 128], P('blk')
Inputs may be any that keep to these rules, and one draw needn't show every extreme that they name: positions is a permutation of 0 to 8191; row r holds position (r mod 512) * 16 + sigma(r div 512), sigma a permutation of the blocks of 512 rows. doc_start of a row is the first position of the document that holds the row's position; documents are runs of consecutive positions, the first starting at 0, and the last position starts a document of its own.
All inputs are finite; a program needn't handle non-finite values.
Results may differ from a plain program's by a relative error of at most 0.0063.
Values may be sent and summed in bfloat16 or wider, within the bound.
A program may use at most 64 MiB of HBM per device.

v0:
```python
import jax
import jax.numpy as jnp
from jax import lax
from jax.sharding import PartitionSpec as P

STEPS = 4


def from_behind(block, axis, distance):
    devices = range(lax.axis_size(axis))
    route = [((i - distance) % len(devices), i) for i in devices]
    return lax.ppermute(block, axis, route)


def block_grads(
    queries,
    out_grad,
    logsumexp,
    row_delta,
    query_places,
    query_starts,
    key_vectors,
    value_vectors,
    key_places,
):
    scaling = queries.shape[-1] ** (-0.5)
    scores = (
        jnp.einsum("thd,kd->htk", queries, key_vectors, preferred_element_type=jnp.float32)
        * scaling
    )
    allowed = (key_places[None, :] <= query_places[:, None]) & (
        key_places[None, :] >= query_starts[:, None]
    )
    attend = jnp.where(allowed[None], jnp.exp(scores - logsumexp.T[:, :, None]), 0.0)
    attend_low = attend.astype(jnp.bfloat16)
    attend_grad = jnp.einsum(
        "thd,kd->htk", out_grad, value_vectors, preferred_element_type=jnp.float32
    )
    score_grad = attend * (attend_grad - row_delta.T[:, :, None])
    score_low = score_grad.astype(jnp.bfloat16)
    value_part = jnp.einsum("htk,thd->kd", attend_low, out_grad, preferred_element_type=jnp.float32)
    key_part = scaling * jnp.einsum(
        "htk,thd->kd", score_low, queries, preferred_element_type=jnp.float32
    )
    query_part = scaling * jnp.einsum(
        "htk,kd->thd", score_low, key_vectors, preferred_element_type=jnp.float32
    )
    return (query_part, key_part, value_part)


def on_device(
    queries, out_grad, outputs, key_vectors, value_vectors, logsumexp, positions, doc_start
):
    row_delta = jnp.sum(out_grad.astype(jnp.float32) * outputs.astype(jnp.float32), axis=-1)
    query_places = positions.astype(jnp.float32)
    query_starts = doc_start.astype(jnp.float32)
    key_zeros = jnp.zeros(key_vectors.shape, jnp.float32)
    guest_keys, guest_values = (key_vectors, value_vectors)
    carried = (key_zeros, key_zeros, query_places)
    query_total = jnp.zeros(queries.shape, jnp.float32)
    for cycle_step in range(STEPS):
        if cycle_step > 0:
            guest_keys, guest_values = from_behind((guest_keys, guest_values), "blk", -1)
            carried = from_behind((carried[0], carried[1], carried[2]), "blk", -1)
        query_part, key_part, value_part = block_grads(
            queries,
            out_grad,
            logsumexp,
            row_delta,
            query_places,
            query_starts,
            guest_keys,
            guest_values,
            carried[2],
        )
        query_total = query_total + query_part
        carried = (carried[0] + key_part, carried[1] + value_part, carried[2])
    key_total, value_total = from_behind((carried[0], carried[1]), "blk", STEPS - 1)
    key_total, value_total = lax.psum((key_total, value_total), "head")
    key_grad = key_total.astype(jnp.bfloat16)
    value_grad = value_total.astype(jnp.bfloat16)
    return (query_total.astype(jnp.bfloat16), key_grad, value_grad)


def solution(mesh):
    in_specs = (
        P("blk", "head", None),
        P("blk", "head", None),
        P("blk", "head", None),
        P("blk", None),
        P("blk", None),
        P("blk", "head"),
        P("blk"),
        P("blk"),
    )
    out_specs = (P("blk", "head", None), P("blk", None), P("blk", None))
    return jax.shard_map(
        on_device, mesh=mesh, in_specs=in_specs, out_specs=out_specs, check_vma=False
    )
```

profile of v0, /device:TPU:1, one launch (start us, length us, event | category | flops | bytes accessed | tf_op | source)
XLA Modules:
  0.0 119.1 jit_solution(15478278479440468709)
XLA Ops:
  1.5 5.5 %collective-permute-start.1 = (bf16[512,128]{1,0:T(8,128)(2,1)}, bf16[512,128]{1,0:T(8,128)(2,1)S(1)}, u32[]{:S(2)}, u32[]{:S(2)}) collective-permute-start(bf16[512,128]{1,0:T(8,128)(2,1)} %param.11), channel_id=1, source_target_pairs={{2,0},{4,2},{6,4},{8,6},{10,8},{12,10},{14,12},{16,14},{18,16},{20... | collective-permute-start | bytes 393224 | tf_op jit(solution)/shard_map/ppermute | solution.py:12
  8.3 5.4 %fusion.77 = f32[512,512,8]{1,0,2:T(8,128)} fusion(bf16[512,8,128]{2,1,0:T(8,128)(2,1)S(1)} %copy-done, bf16[512,128]{1,0:T(8,128)(2,1)} %param.11), kind=kOutput, calls=%fused_computation.77 | convolution fusion | flops 536870912 | bytes 9568256 | tf_op jit(solution)/shard_map/thd,kd->htk/dot_general | solution.py:28
  13.8 4.4 %collective-permute-start.6 = (f32[512]{0:T(512)S(1)}, f32[512]{0:T(512)S(1)}, u32[]{:S(2)}, u32[]{:S(2)}) collective-permute-start(f32[512]{0:T(512)S(1)} %collective-permute-done.3), channel_id=1, source_target_pairs={{2,0},{4,2},{6,4},{8,6},{10,8},{12,10},{14,12},{16,14},{18,16},{20... | collective-permute-start | bytes 6152 | tf_op jit(solution)/shard_map/ppermute | solution.py:12
  19.9 6.2 %fusion.38 = f32[512,128]{1,0:T(8,128)} fusion(f32[512,512,8]{1,0,2:T(8,128)} %fusion.77, f32[8,512]{1,0:T(8,128)S(1)} %bitcast.159, pred[512,512]{0,1:T(8,128)(4,1)S(1)} %get-tuple-element.14, bf16[512,8,128]{2,1,0:T(8,128)(2,1)} %param.9), kind=kOutput, calls=%fused_computation.48 | convolution fusion | flops 545259520 | bytes 9977856 | tf_op jit(solution)/shard_map/htk,thd->kd/dot_general | solution.py:41
  26.1 5.2 %fusion.13 = bf16[8,512,512]{1,2,0:T(8,128)(2,1)S(1)} fusion(f32[512,512,8]{1,0,2:T(8,128)} %fusion.77, f32[8,512]{1,0:T(8,128)S(1)} %copy.34, f32[8,512]{1,0:T(8,128)S(1)} %bitcast.160, pred[512,512]{0,1:T(8,128)(4,1)S(1)} %get-tuple-element.14, bf16[512,8,128]{2,1,0:T(8,128)(2,1)S(1)} %copy-done.3, bf16[512,128]{1,0:T(8,128)(2,1)S(1)} %copy-done.12), kind=kOutput, calls=%fused_computation.20 | convolution fusion | flops 549453824 | bytes 14057472 | tf_op jit(solution)/shard_map/thd,kd->htk/dot_general | solution.py:36
  31.3 2.0 %fusion.33 = f32[512,128]{1,0:T(8,128)} fusion(bf16[8,512,512]{1,2,0:T(8,128)(2,1)S(1)} %fusion.13, bf16[512,8,128]{2,1,0:T(8,128)(2,1)S(1)} %copy-done), kind=kOutput, calls=%fused_computation.43 | convolution fusion | flops 536936448 | bytes 5505024 | tf_op jit(solution)/shard_map/htk,thd->kd/dot_general | solution.py:42
  33.3 1.3 %fusion.91 = f32[8,512,128]{2,1,0:T(8,128)S(1)} fusion(bf16[8,512,512]{1,2,0:T(8,128)(2,1)S(1)} %fusion.13, bf16[512,128]{1,0:T(8,128)(2,1)S(1)} %copy-done.5), kind=kOutput, calls=%fused_computation.91 | convolution fusion | flops 536870912 | bytes 6422528 | tf_op jit(solution)/shard_map/htk,kd->thd/dot_general | solution.py:45
  35.3 4.4 %collective-permute-start.13 = (f32[512,128]{1,0:T(8,128)}, f32[512,128]{1,0:T(8,128)}, u32[]{:S(2)}, u32[]{:S(2)}) collective-permute-start(f32[512,128]{1,0:T(8,128)} %fusion.38), channel_id=1, source_target_pairs={{2,0},{4,2},{6,4},{8,6},{10,8},{12,10},{14,12},{16,14},{18,16},{20... | collective-permute-start | bytes 786440 | tf_op jit(solution)/shard_map/ppermute | solution.py:12
  39.8 1.3 %fusion.75 = f32[512,512,8]{1,0,2:T(8,128)S(1)} fusion(bf16[512,8,128]{2,1,0:T(8,128)(2,1)S(1)} %copy-done, bf16[512,128]{1,0:T(8,128)(2,1)S(1)} %collective-permute-done.1), kind=kOutput, calls=%fused_computation.75 | convolution fusion | flops 536870912 | bytes 9568256 | tf_op jit(solution)/shard_map/thd,kd->htk/dot_general | solution.py:28
  41.4 4.0 %fusion.9 = bf16[8,512,512]{1,2,0:T(8,128)(2,1)S(1)} fusion(f32[512,512,8]{1,0,2:T(8,128)S(1)} %fusion.75, f32[8,512]{1,0:T(8,128)S(1)} %copy.34, f32[8,512]{1,0:T(8,128)S(1)} %bitcast.161, pred[512,512]{0,1:T(8,128)(4,1)S(1)} %get-tuple-element.11, bf16[512,8,128]{2,1,0:T(8,128)(2,1)S(1)} %copy-done.4, bf16[512,128]{1,0:T(8,128)(2,1)} %collective-permute-done.2), kind=kOutput, calls=%fused_computation.14 | convolution fusion | flops 549453824 | bytes 14057472 | tf_op jit(solution)/shard_map/thd,kd->htk/dot_general | solution.py:36
  45.4 1.3 %fusion.87 = f32[8,512,128]{2,1,0:T(8,128)S(1)} fusion(bf16[8,512,512]{1,2,0:T(8,128)(2,1)S(1)} %fusion.9, bf16[512,128]{1,0:T(8,128)(2,1)S(1)} %collective-permute-done.1), kind=kOutput, calls=%fused_computation.87 | convolution fusion | flops 536870912 | bytes 6422528 | tf_op jit(solution)/shard_map/htk,kd->thd/dot_general | solution.py:45
  46.7 1.3 %fusion.73 = f32[512,512,8]{1,0,2:T(8,128)S(1)} fusion(bf16[512,8,128]{2,1,0:T(8,128)(2,1)S(1)} %copy-done, bf16[512,128]{1,0:T(8,128)(2,1)S(1)} %collective-permute-done.4), kind=kOutput, calls=%fused_computation.73 | convolution fusion | flops 536870912 | bytes 9568256 | tf_op jit(solution)/shard_map/thd,kd->htk/dot_general | solution.py:28
  48.0 5.3 %fusion.5 = bf16[8,512,512]{1,2,0:T(8,128)(2,1)} fusion(f32[512,512,8]{1,0,2:T(8,128)S(1)} %fusion.73, f32[8,512]{1,0:T(8,128)S(1)} %copy.34, f32[8,512]{1,0:T(8,128)S(1)} %bitcast.162, pred[512,512]{0,1:T(8,128)(4,1)S(1)} %get-tuple-element.12, bf16[512,8,128]{2,1,0:T(8,128)(2,1)S(1)} %copy-done.4, bf16[512,128]{1,0:T(8,128)(2,1)} %collective-permute-done.5), kind=kOutput, calls=%fused_computation.8 | convolution fusion | flops 549453824 | bytes 14057472 | tf_op jit(solution)/shard_map/thd,kd->htk/dot_general | solution.py:36
  53.3 3.5 %fusion.36 = f32[512,128]{1,0:T(8,128)S(1)} fusion(bf16[8,512,512]{1,2,0:T(8,128)(2,1)} %fusion.5, bf16[512,8,128]{2,1,0:T(8,128)(2,1)S(1)} %copy-done), kind=kOutput, calls=%fused_computation.46 | convolution fusion | flops 536936448 | bytes 5505024 | tf_op jit(solution)/shard_map/htk,thd->kd/dot_general | solution.py:42
  56.8 1.6 %collective-permute-start.7 = (bf16[512,128]{1,0:T(8,128)(2,1)S(1)}, bf16[512,128]{1,0:T(8,128)(2,1)S(1)}, u32[]{:S(2)}, u32[]{:S(2)}) collective-permute-start(bf16[512,128]{1,0:T(8,128)(2,1)S(1)} %collective-permute-done.4), channel_id=1, source_target_pairs={{2,0},{4,2},{6,4},{8,6},{10,8},{12,10},{14,12},{16,14},{18,16},{20... | collective-permute-start | bytes 393224 | tf_op jit(solution)/shard_map/ppermute | solution.py:12
  58.4 4.6 %collective-permute-start.8 = (bf16[512,128]{1,0:T(8,128)(2,1)}, bf16[512,128]{1,0:T(8,128)(2,1)S(1)}, u32[]{:S(2)}, u32[]{:S(2)}) collective-permute-start(bf16[512,128]{1,0:T(8,128)(2,1)} %collective-permute-done.5), channel_id=1, source_target_pairs={{2,0},{4,2},{6,4},{8,6},{10,8},{12,10},{14,12},{16,14},{18,16},{20... | collective-permute-start | bytes 393224 | tf_op jit(solution)/shard_map/ppermute | solution.py:12
  63.0 3.5 %fusion.83 = f32[8,512,128]{2,1,0:T(8,128)S(1)} fusion(bf16[8,512,512]{1,2,0:T(8,128)(2,1)} %fusion.5, bf16[512,128]{1,0:T(8,128)(2,1)S(1)} %collective-permute-done.4), kind=kOutput, calls=%fused_computation.83 | convolution fusion | flops 536870912 | bytes 6422528 | tf_op jit(solution)/shard_map/htk,kd->thd/dot_general | solution.py:45
  66.5 2.9 %fusion.35 = f32[512,128]{1,0:T(8,128)} fusion(f32[512,128]{1,0:T(8,128)} %collective-permute-done.9, bf16[8,512,512]{1,2,0:T(8,128)(2,1)S(1)} %fusion.9, bf16[512,8,128]{2,1,0:T(8,128)(2,1)S(1)} %copy-done), kind=kOutput, calls=%fused_computation.45 | convolution fusion | flops 537001984 | bytes 5767168 | tf_op jit(solution)/shard_map/htk,thd->kd/dot_general | solution.py:42
  69.5 3.6 %fusion.56 = f32[512,128]{1,0:T(8,128)} fusion(f32[512,128]{1,0:T(8,128)} %collective-permute-done.13, f32[512,512,8]{1,0,2:T(8,128)S(1)} %fusion.75, f32[8,512]{1,0:T(8,128)S(1)} %bitcast.163, pred[512,512]{0,1:T(8,128)(4,1)S(1)} %copy-done.10, bf16[512,8,128]{2,1,0:T(8,128)(2,1)S(1)} %copy-done.4), kind=kOutput, calls=%fused_computation.54 | convolution fusion | flops 545325056 | bytes 10240000 | tf_op jit(solution)/shard_map/htk,thd->kd/dot_general | solution.py:41
  73.1 1.3 %fusion.71 = f32[512,512,8]{1,0,2:T(8,128)S(1)} fusion(bf16[512,8,128]{2,1,0:T(8,128)(2,1)S(1)} %copy-done, bf16[512,128]{1,0:T(8,128)(2,1)S(1)} %collective-permute-done.7), kind=kOutput, calls=%fused_computation.71 | convolution fusion | flops 536870912 | bytes 9568256 | tf_op jit(solution)/shard_map/thd,kd->htk/dot_general | solution.py:28
  75.0 4.0 %fusion.1 = bf16[8,512,512]{1,2,0:T(8,128)(2,1)S(1)} fusion(f32[512,512,8]{1,0,2:T(8,128)S(1)} %fusion.71, f32[8,512]{1,0:T(8,128)S(1)} %copy.34, f32[8,512]{1,0:T(8,128)S(1)} %bitcast.164, pred[512,512]{0,1:T(8,128)(4,1)S(1)} %get-tuple-element.13, bf16[512,8,128]{2,1,0:T(8,128)(2,1)S(1)} %copy-done.4, bf16[512,128]{1,0:T(8,128)(2,1)} %copy-done.13), kind=kOutput, calls=%fused_computation.2 | convolution fusion | flops 549453824 | bytes 14057472 | tf_op jit(solution)/shard_map/thd,kd->htk/dot_general | solution.py:36
  79.2 2.9 %fusion.53 = f32[512,128]{1,0:T(8,128)S(1)} fusion(f32[512,128]{1,0:T(8,128)} %collective-permute-done.14, f32[512,512,8]{1,0,2:T(8,128)S(1)} %fusion.73, f32[8,512]{1,0:T(8,128)S(1)} %bitcast.165, pred[512,512]{0,1:T(8,128)(4,1)} %copy-done.8, bf16[512,8,128]{2,1,0:T(8,128)(2,1)S(1)} %copy-done.4), kind=kOutput, calls=%fused_computation.53 | convolution fusion | flops 545325056 | bytes 10240000 | tf_op jit(solution)/shard_map/htk,thd->kd/dot_general | solution.py:41
  82.2 1.2 %fusion.37 = f32[512,128]{1,0:T(8,128)S(1)} fusion(bf16[8,512,512]{1,2,0:T(8,128)(2,1)S(1)} %fusion.1, bf16[512,8,128]{2,1,0:T(8,128)(2,1)S(1)} %copy-done), kind=kOutput, calls=%fused_computation.47 | convolution fusion | flops 536936448 | bytes 5505024 | tf_op jit(solution)/shard_map/htk,thd->kd/dot_general | solution.py:42
  83.4 1.5 %collective-permute-done.11 = f32[512,128]{1,0:T(8,128)S(1)} collective-permute-done((f32[512,128]{1,0:T(8,128)S(1)}, f32[512,128]{1,0:T(8,128)S(1)}, u32[]{:S(2)}, u32[]{:S(2)}) %collective-permute-start.11) | collective-permute-done | bytes 262176 | tf_op jit(solution)/shard_map/ppermute | solution.py:12
  85.0 1.8 %collective-permute-start.12 = (f32[512,128]{1,0:T(8,128)S(1)}, f32[512,128]{1,0:T(8,128)S(1)}, u32[]{:S(2)}, u32[]{:S(2)}) collective-permute-start(f32[512,128]{1,0:T(8,128)S(1)} %add.42), channel_id=1, source_target_pairs={{26,0},{28,2},{30,4},{0,6},{2,8},{4,10},{6,12},{8,14},{10,16},{12,... | collective-permute-start | bytes 786440 | tf_op jit(solution)/shard_map/ppermute | solution.py:12
  86.8 1.1 collective-permute-done.15
  88.0 1.9 %fusion.50 = f32[512,128]{1,0:T(8,128)S(1)} fusion(f32[512,128]{1,0:T(8,128)S(1)} %collective-permute-done.15, f32[512,512,8]{1,0,2:T(8,128)S(1)} %fusion.71, f32[8,512]{1,0:T(8,128)S(1)} %bitcast.166, pred[512,512]{0,1:T(8,128)(4,1)S(1)} %copy-done.7, bf16[512,8,128]{2,1,0:T(8,128)(2,1)S(1)} %copy-done.4), kind=kOutput, calls=%fused_computation.52 | convolution fusion | flops 545325056 | bytes 10240000 | tf_op jit(solution)/shard_map/htk,thd->kd/dot_general | solution.py:41
  89.9 1.4 %collective-permute-start.16 = (f32[512,128]{1,0:T(8,128)S(1)}, f32[512,128]{1,0:T(8,128)}, u32[]{:S(2)}, u32[]{:S(2)}) collective-permute-start(f32[512,128]{1,0:T(8,128)S(1)} %fusion.50), channel_id=1, source_target_pairs={{26,0},{28,2},{30,4},{0,6},{2,8},{4,10},{6,12},{8,14},{10,16},{12,... | collective-permute-start | bytes 786440 | tf_op jit(solution)/shard_map/ppermute | solution.py:12
  91.3 1.4 %fusion.32 = bf16[512,8,128]{2,0,1:T(8,128)(2,1)S(1)} fusion(bf16[8,512,512]{1,2,0:T(8,128)(2,1)S(1)} %fusion.1, f32[8,512,128]{2,1,0:T(8,128)S(1)} %fusion.83, f32[8,512,128]{2,1,0:T(8,128)S(1)} %fusion.91, f32[8,512,128]{2,1,0:T(8,128)S(1)} %fusion.87, bf16[512,128]{1,0:T(8,128)(2,1)S(1)} %collective-permute-done.7), kind=kOutput, calls=%fused_computation.38 | convolution fusion | flops 539492352 | bytes 11665408 | tf_op jit(solution)/shard_map/htk,kd->thd/dot_general | solution.py:45
  92.7 1.7 %copy.53 = bf16[512,8,128]{2,1,0:T(8,128)(2,1)} copy(bf16[512,8,128]{2,0,1:T(8,128)(2,1)S(1)} %fusion.32) | data formatting | bytes 2097152
  94.8 5.2 %collective-permute-done.16 = f32[512,128]{1,0:T(8,128)} collective-permute-done((f32[512,128]{1,0:T(8,128)S(1)}, f32[512,128]{1,0:T(8,128)}, u32[]{:S(2)}, u32[]{:S(2)}) %collective-permute-start.16) | collective-permute-done | bytes 262176 | tf_op jit(solution)/shard_map/ppermute | solution.py:12
  100.0 19.1 %all-reduce.2 = (bf16[512,128]{1,0:T(8,128)(2,1)}, bf16[512,128]{1,0:T(8,128)(2,1)}) all-reduce(f32[512,128]{1,0:T(8,128)S(1)} %collective-permute-done.12, f32[512,128]{1,0:T(8,128)} %collective-permute-done.16), channel_id=1, replica_groups=mesh['blk'=16,'head'=2] {'head'}, use_global_device_ids=true, to_apply=%region_1.2 | all-reduce | flops 131072 | bytes 786432 | tf_op jit(solution)/shard_map/psum | solution.py:79
  (67 shorter events, 6.5 us)
Async XLA Ops:
  0.6 7.7 %copy-start = (bf16[512,8,128]{2,1,0:T(8,128)(2,1)S(1)}, bf16[512,8,128]{2,1,0:T(8,128)(2,1)}, u32[]{:S(2)}) copy-start(bf16[512,8,128]{2,1,0:T(8,128)(2,1)} %param.8) | copy-start | bytes 3145732
  0.6 17.5 %copy-start.1 = (bf16[512,8,128]{2,1,0:T(8,128)(2,1)S(1)}, bf16[512,8,128]{2,1,0:T(8,128)(2,1)}, u32[]{:S(2)}) copy-start(bf16[512,8,128]{2,1,0:T(8,128)(2,1)} %param.10) | copy-start | bytes 3145732
  0.7 17.5 %copy-start.2 = (bf16[512,8,128]{2,1,0:T(8,128)(2,1)S(1)}, bf16[512,8,128]{2,1,0:T(8,128)(2,1)}, u32[]{:S(2)}) copy-start(bf16[512,8,128]{2,1,0:T(8,128)(2,1)} %param.9) | copy-start | bytes 3145732
  0.7 18.1 %copy-start.11 = (s32[512]{0:T(512)S(1)}, s32[512]{0:T(512)}, u32[]{:S(2)}) copy-start(s32[512]{0:T(512)} %param.15) | copy-start | bytes 6148
  0.7 19.2 %copy-start.14 = (f32[512,8]{0,1:T(8,128)S(1)}, f32[512,8]{0,1:T(8,128)}, u32[]{:S(2)}) copy-start(f32[512,8]{0,1:T(8,128)} %param.13) | copy-start | bytes 49156
  1.5 6.2 %collective-permute-start = (f32[512]{0:T(512)S(1)}, f32[512]{0:T(512)S(1)}, u32[]{:S(2)}, u32[]{:S(2)}) collective-permute-start(f32[512]{0:T(512)S(1)} %convert_element_type.43), channel_id=1, source_target_pairs={{2,0},{4,2},{6,4},{8,6},{10,8},{12,10},{14,12},{16,14},{18,16},{20... | collective-permute-start | bytes 6152 | tf_op jit(solution)/shard_map/ppermute | solution.py:12
  1.5 38.2 %collective-permute-start.1 = (bf16[512,128]{1,0:T(8,128)(2,1)}, bf16[512,128]{1,0:T(8,128)(2,1)S(1)}, u32[]{:S(2)}, u32[]{:S(2)}) collective-permute-start(bf16[512,128]{1,0:T(8,128)(2,1)} %param.11), channel_id=1, source_target_pairs={{2,0},{4,2},{6,4},{8,6},{10,8},{12,10},{14,12},{16,14},{18,16},{20... | collective-permute-start | bytes 393224 | tf_op jit(solution)/shard_map/ppermute | solution.py:12
  7.0 34.1 %collective-permute-start.2 = (bf16[512,128]{1,0:T(8,128)(2,1)}, bf16[512,128]{1,0:T(8,128)(2,1)}, u32[]{:S(2)}, u32[]{:S(2)}) collective-permute-start(bf16[512,128]{1,0:T(8,128)(2,1)} %param.12), channel_id=1, source_target_pairs={{2,0},{4,2},{6,4},{8,6},{10,8},{12,10},{14,12},{16,14},{18,16},{20... | collective-permute-start | bytes 393224 | tf_op jit(solution)/shard_map/ppermute | solution.py:12
  7.7 6.1 %collective-permute-start.3 = (f32[512]{0:T(512)S(1)}, f32[512]{0:T(512)S(1)}, u32[]{:S(2)}, u32[]{:S(2)}) collective-permute-start(f32[512]{0:T(512)S(1)} %collective-permute-done), channel_id=1, source_target_pairs={{2,0},{4,2},{6,4},{8,6},{10,8},{12,10},{14,12},{16,14},{18,16},{20... | collective-permute-start | bytes 6152 | tf_op jit(solution)/shard_map/ppermute | solution.py:12
  13.8 5.2 %collective-permute-start.6 = (f32[512]{0:T(512)S(1)}, f32[512]{0:T(512)S(1)}, u32[]{:S(2)}, u32[]{:S(2)}) collective-permute-start(f32[512]{0:T(512)S(1)} %collective-permute-done.3), channel_id=1, source_target_pairs={{2,0},{4,2},{6,4},{8,6},{10,8},{12,10},{14,12},{16,14},{18,16},{20... | collective-permute-start | bytes 6152 | tf_op jit(solution)/shard_map/ppermute | solution.py:12
  18.8 7.3 %copy-start.3 = (bf16[512,8,128]{2,1,0:T(8,128)(2,1)S(1)}, bf16[512,8,128]{2,1,0:T(8,128)(2,1)}, u32[]{:S(2)}) copy-start(bf16[512,8,128]{2,1,0:T(8,128)(2,1)} %param.9) | copy-start | bytes 3145732
  19.9 21.5 %copy-start.9 = (pred[512,512]{0,1:T(8,128)(4,1)}, pred[512,512]{0,1:T(8,128)(4,1)S(1)}, u32[]{:S(2)}) copy-start(pred[512,512]{0,1:T(8,128)(4,1)S(1)} %get-tuple-element.11) | copy-start | bytes 786436
  19.9 28.1 %copy-start.8 = (pred[512,512]{0,1:T(8,128)(4,1)}, pred[512,512]{0,1:T(8,128)(4,1)S(1)}, u32[]{:S(2)}) copy-start(pred[512,512]{0,1:T(8,128)(4,1)S(1)} %get-tuple-element.12) | copy-start | bytes 786436
  19.9 55.1 %copy-start.6 = (pred[512,512]{0,1:T(8,128)(4,1)}, pred[512,512]{0,1:T(8,128)(4,1)S(1)}, u32[]{:S(2)}) copy-start(pred[512,512]{0,1:T(8,128)(4,1)S(1)} %get-tuple-element.13) | copy-start | bytes 786436
  33.3 8.1 %copy-start.4 = (bf16[512,8,128]{2,1,0:T(8,128)(2,1)S(1)}, bf16[512,8,128]{2,1,0:T(8,128)(2,1)}, u32[]{:S(2)}) copy-start(bf16[512,8,128]{2,1,0:T(8,128)(2,1)} %param.9) | copy-start | bytes 3145732
  33.3 8.1 %copy-start.15 = (f32[512,8]{0,1:T(8,128)S(1)}, f32[512,8]{0,1:T(8,128)}, u32[]{:S(2)}) copy-start(f32[512,8]{0,1:T(8,128)} %param.13) | copy-start | bytes 49156
  34.6 31.9 %collective-permute-start.9 = (f32[512,128]{1,0:T(8,128)}, f32[512,128]{1,0:T(8,128)}, u32[]{:S(2)}, u32[]{:S(2)}) collective-permute-start(f32[512,128]{1,0:T(8,128)} %fusion.33), channel_id=1, source_target_pairs={{2,0},{4,2},{6,4},{8,6},{10,8},{12,10},{14,12},{16,14},{18,16},{20... | collective-permute-start | bytes 786440 | tf_op jit(solution)/shard_map/ppermute | solution.py:12
  35.3 34.1 %collective-permute-start.13 = (f32[512,128]{1,0:T(8,128)}, f32[512,128]{1,0:T(8,128)}, u32[]{:S(2)}, u32[]{:S(2)}) collective-permute-start(f32[512,128]{1,0:T(8,128)} %fusion.38), channel_id=1, source_target_pairs={{2,0},{4,2},{6,4},{8,6},{10,8},{12,10},{14,12},{16,14},{18,16},{20... | collective-permute-start | bytes 786440 | tf_op jit(solution)/shard_map/ppermute | solution.py:12
  41.0 5.7 %collective-permute-start.4 = (bf16[512,128]{1,0:T(8,128)(2,1)S(1)}, bf16[512,128]{1,0:T(8,128)(2,1)S(1)}, u32[]{:S(2)}, u32[]{:S(2)}) collective-permute-start(bf16[512,128]{1,0:T(8,128)(2,1)S(1)} %collective-permute-done.1), channel_id=1, source_target_pairs={{2,0},{4,2},{6,4},{8,6},{10,8},{12,10},{14,12},{16,14},{18,16},{20... | collective-permute-start | bytes 393224 | tf_op jit(solution)/shard_map/ppermute | solution.py:12
  41.1 6.9 %collective-permute-start.5 = (bf16[512,128]{1,0:T(8,128)(2,1)}, bf16[512,128]{1,0:T(8,128)(2,1)}, u32[]{:S(2)}, u32[]{:S(2)}) collective-permute-start(bf16[512,128]{1,0:T(8,128)(2,1)} %collective-permute-done.2), channel_id=1, source_target_pairs={{2,0},{4,2},{6,4},{8,6},{10,8},{12,10},{14,12},{16,14},{18,16},{20... | collective-permute-start | bytes 393224 | tf_op jit(solution)/shard_map/ppermute | solution.py:12
  53.3 16.1 %copy-start.10 = (pred[512,512]{0,1:T(8,128)(4,1)S(1)}, pred[512,512]{0,1:T(8,128)(4,1)}, u32[]{:S(2)}) copy-start(pred[512,512]{0,1:T(8,128)(4,1)} %copy-done.9) | copy-start | bytes 786436
  53.3 16.1 %copy-start.16 = (f32[512,8]{0,1:T(8,128)S(1)}, f32[512,8]{0,1:T(8,128)}, u32[]{:S(2)}) copy-start(f32[512,8]{0,1:T(8,128)} %param.13) | copy-start | bytes 49156
  56.8 16.3 %collective-permute-start.7 = (bf16[512,128]{1,0:T(8,128)(2,1)S(1)}, bf16[512,128]{1,0:T(8,128)(2,1)S(1)}, u32[]{:S(2)}, u32[]{:S(2)}) collective-permute-start(bf16[512,128]{1,0:T(8,128)(2,1)S(1)} %collective-permute-done.4), channel_id=1, source_target_pairs={{2,0},{4,2},{6,4},{8,6},{10,8},{12,10},{14,12},{16,14},{18,16},{20... | collective-permute-start | bytes 393224 | tf_op jit(solution)/shard_map/ppermute | solution.py:12
  58.4 15.9 %collective-permute-start.8 = (bf16[512,128]{1,0:T(8,128)(2,1)}, bf16[512,128]{1,0:T(8,128)(2,1)S(1)}, u32[]{:S(2)}, u32[]{:S(2)}) collective-permute-start(bf16[512,128]{1,0:T(8,128)(2,1)} %collective-permute-done.5), channel_id=1, source_target_pairs={{2,0},{4,2},{6,4},{8,6},{10,8},{12,10},{14,12},{16,14},{18,16},{20... | collective-permute-start | bytes 393224 | tf_op jit(solution)/shard_map/ppermute | solution.py:12
  69.4 9.6 %collective-permute-start.10 = (f32[512,128]{1,0:T(8,128)}, f32[512,128]{1,0:T(8,128)S(1)}, u32[]{:S(2)}, u32[]{:S(2)}) collective-permute-start(f32[512,128]{1,0:T(8,128)} %fusion.35), channel_id=1, source_target_pairs={{2,0},{4,2},{6,4},{8,6},{10,8},{12,10},{14,12},{16,14},{18,16},{20... | collective-permute-start | bytes 786440 | tf_op jit(solution)/shard_map/ppermute | solution.py:12
  73.1 6.1 %collective-permute-start.14 = (f32[512,128]{1,0:T(8,128)}, f32[512,128]{1,0:T(8,128)}, u32[]{:S(2)}, u32[]{:S(2)}) collective-permute-start(f32[512,128]{1,0:T(8,128)} %fusion.56), channel_id=1, source_target_pairs={{2,0},{4,2},{6,4},{8,6},{10,8},{12,10},{14,12},{16,14},{18,16},{20... | collective-permute-start | bytes 786440 | tf_op jit(solution)/shard_map/ppermute | solution.py:12
  79.1 8.9 %copy-start.7 = (pred[512,512]{0,1:T(8,128)(4,1)S(1)}, pred[512,512]{0,1:T(8,128)(4,1)}, u32[]{:S(2)}) copy-start(pred[512,512]{0,1:T(8,128)(4,1)} %copy-done.6) | copy-start | bytes 786436
  79.1 8.9 %copy-start.17 = (f32[512,8]{0,1:T(8,128)S(1)}, f32[512,8]{0,1:T(8,128)}, u32[]{:S(2)}) copy-start(f32[512,8]{0,1:T(8,128)} %param.13) | copy-start | bytes 49156
  79.1 5.9 %collective-permute-start.11 = (f32[512,128]{1,0:T(8,128)S(1)}, f32[512,128]{1,0:T(8,128)S(1)}, u32[]{:S(2)}, u32[]{:S(2)}) collective-permute-start(f32[512,128]{1,0:T(8,128)S(1)} %add.41), channel_id=1, source_target_pairs={{2,0},{4,2},{6,4},{8,6},{10,8},{12,10},{14,12},{16,14},{18,16},{20... | collective-permute-start | bytes 786440 | tf_op jit(solution)/shard_map/ppermute | solution.py:12
  82.1 5.9 %collective-permute-start.15 = (f32[512,128]{1,0:T(8,128)S(1)}, f32[512,128]{1,0:T(8,128)S(1)}, u32[]{:S(2)}, u32[]{:S(2)}) collective-permute-start(f32[512,128]{1,0:T(8,128)S(1)} %fusion.53), channel_id=1, source_target_pairs={{2,0},{4,2},{6,4},{8,6},{10,8},{12,10},{14,12},{16,14},{18,16},{20... | collective-permute-start | bytes 786440 | tf_op jit(solution)/shard_map/ppermute | solution.py:12
  85.0 9.8 %collective-permute-start.12 = (f32[512,128]{1,0:T(8,128)S(1)}, f32[512,128]{1,0:T(8,128)S(1)}, u32[]{:S(2)}, u32[]{:S(2)}) collective-permute-start(f32[512,128]{1,0:T(8,128)S(1)} %add.42), channel_id=1, source_target_pairs={{26,0},{28,2},{30,4},{0,6},{2,8},{4,10},{6,12},{8,14},{10,16},{12,... | collective-permute-start | bytes 786440 | tf_op jit(solution)/shard_map/ppermute | solution.py:12
  89.9 10.1 %collective-permute-start.16 = (f32[512,128]{1,0:T(8,128)S(1)}, f32[512,128]{1,0:T(8,128)}, u32[]{:S(2)}, u32[]{:S(2)}) collective-permute-start(f32[512,128]{1,0:T(8,128)S(1)} %fusion.50), channel_id=1, source_target_pairs={{26,0},{28,2},{30,4},{0,6},{2,8},{4,10},{6,12},{8,14},{10,16},{12,... | collective-permute-start | bytes 786440 | tf_op jit(solution)/shard_map/ppermute | solution.py:12
  (3 other events, 15.1 us)
where the time goes:
time: 120 us; the launch traced here: 119 us
  matrix products  59.4 us (50%)
  starting transfers between devices  26.4 us (22%)
  blocking collectives  19.1 us (16%)
  waiting for transfers between devices  8.36 us (7%)
  local copies, waits for them, and re-layouts  2.48 us (2%)
  other arithmetic  2.42 us (2%)
    ppermute x17, starting transfers between devices, from_behind(): return lax.ppermute(block, axis, route)  26.4 us
    psum x1, blocking collectives, on_device(): key_total, value_total = lax.psum((key_total, value_total), 'head')  19.1 us
    dot_general x4, matrix products, block_grads(): jnp.einsum('thd,kd->htk', out_grad, value_vectors, preferred_element_type...  18.5 us
    dot_general x4, matrix products, block_grads(): jnp.einsum('htk,thd->kd', attend_low, out_grad, preferred_element_type=jn...  14.6 us
    dot_general x4, matrix products, block_grads(): jnp.einsum('htk,thd->kd', score_low, queries, preferred_element_type=jnp....  9.58 us
    dot_general x4, matrix products, block_grads(): jnp.einsum('thd,kd->htk', queries, key_vectors, preferred_element_type=jn...  9.2 us
    ppermute x17, waiting for transfers between devices, from_behind(): return lax.ppermute(block, axis, route)  8.36 us
    dot_general x4, matrix products, block_grads(): jnp.einsum('htk,kd->thd', score_low, key_vectors, preferred_element_type=...  7.46 us
  transfers between devices with their start and end apart: 17, of which 4 were waited for; matrix products, arithmetic and copies ran while one was open for 53% of the time, Pallas kernels for 0%

commit v1 on v0

v1 whole, which is shorter than its diff:
```python
import functools
import math

import jax
import jax.numpy as jnp
from jax import lax
from jax.experimental import pallas as pl
from jax.experimental.pallas import tpu as pltpu
from jax.sharding import PartitionSpec as P

STEPS = 4
TILE = 64
CHUNKS = 4
LOG2E = math.log2(math.e)
MESH = pl.DeviceIdType.MESH
VMEM_SPEC = pl.BlockSpec(memory_space=pltpu.VMEM)


def places(n):
    b = lax.axis_index("blk")
    h = lax.axis_index("head")
    even = lax.rem(b, 2) == 0
    partner = jnp.where(even, b + 1, b - 1)

    def at(d):
        return lax.rem(b + d + n, n)

    return b, h, even, partner, at


def greet(n):
    b, h, even, partner, at = places(n)
    barrier = pltpu.get_barrier_semaphore()
    for d in (-3, -2, -1, 1, 2, 3):
        pl.semaphore_signal(barrier, inc=1, device_id=(at(d), h), device_id_type=MESH)
    pl.semaphore_signal(barrier, inc=1, device_id=(b, 1 - h), device_id_type=MESH)
    pl.semaphore_wait(barrier, 7)


def gather_kernel(n, k_ref, v_ref, pos_ref, kall, vall, pos_all, send, recv, local):
    b, h, even, partner, at = places(n)
    rows = k_ref.shape[0]
    half = rows // 2
    mine = pl.ds(pl.multiple_of(h * half, half), half)
    other = pl.ds(pl.multiple_of((1 - h) * half, half), half)
    pairs = ((k_ref, kall), (v_ref, vall))

    def copy(src, dst, kind, j, who):
        return pltpu.make_async_remote_copy(
            src_ref=src,
            dst_ref=dst,
            send_sem=send.at[kind, j],
            recv_sem=recv.at[kind, j],
            device_id=who,
            device_id_type=MESH,
        )

    own = [
        pltpu.make_async_copy(src, dst.at[0], local.at[j])
        for j, (src, dst) in enumerate(pairs + ((pos_ref, pos_all),))
    ]
    for c in own:
        c.start()
    greet(n)
    pslot = jnp.where(even, 1, 3)
    qslot = jnp.where(even, 3, 1)
    first, third, near = [], [], []
    for j, (src, dst) in enumerate(pairs):
        first.append(copy(src.at[mine], dst.at[2, mine], 0, j, (at(-2), h)))
        third.append(copy(src.at[mine], dst.at[3, mine], 1, j, (at(-3), h)))
        near.append(copy(src, dst.at[1], 2, j, (partner, h)))
    for j in range(2):
        first[j].start()

        @pl.when(even)
        def _():
            third[j].start()

        @pl.when(jnp.logical_not(even))
        def _():
            near[j].start()

    marks = [
        copy(pos_ref, pos_all.at[d], 7 + d // 3, d % 3, (at(-d), h)) for d in range(1, STEPS)
    ]
    for c in marks:
        c.start()

    side, side3, fwd, fwd2 = [], [], [], []
    for j, (src, dst) in enumerate(pairs):
        side.append(copy(dst.at[2, mine], dst.at[2, mine], 3, j, (b, 1 - h)))
        side3.append(copy(dst.at[3, mine], dst.at[3, mine], 4, j, (b, 1 - h)))
        fwd.append(copy(dst.at[2, mine], dst.at[pslot, mine], 5, j, (partner, h)))
        fwd2.append(copy(dst.at[2, other], dst.at[pslot, other], 6, j, (partner, h)))
    for j in range(2):
        first[j].wait_recv()
        side[j].start()
        fwd[j].start()
    for j in range(2):

        @pl.when(jnp.logical_not(even))
        def _():
            third[j].wait_recv()
            side3[j].start()

    for j in range(2):
        side[j].wait_recv()
        fwd2[j].start()
    for j in range(2):
        fwd[j].wait_recv()
        fwd2[j].wait_recv()

        @pl.when(even)
        def _():
            near[j].wait_recv()
            third[j].wait_send()

        @pl.when(jnp.logical_not(even))
        def _():
            side3[j].wait_recv()
            near[j].wait_send()
            side3[j].wait_send()

        first[j].wait_send()
        side[j].wait_send()
        fwd[j].wait_send()
        fwd2[j].wait_send()
    for c in own + marks:
        c.wait()


def gather(n, keys, values, marks):
    rows, width = keys.shape
    shape = jax.ShapeDtypeStruct((STEPS, rows, width), keys.dtype)
    mark = jax.ShapeDtypeStruct((STEPS,) + marks.shape, marks.dtype)
    return pl.pallas_call(
        functools.partial(gather_kernel, n),
        out_shape=(shape, shape, mark),
        in_specs=[VMEM_SPEC] * 3,
        out_specs=(VMEM_SPEC,) * 3,
        scratch_shapes=[
            pltpu.SemaphoreType.DMA((9, 3)),
            pltpu.SemaphoreType.DMA((9, 3)),
            pltpu.SemaphoreType.DMA((3,)),
        ],
        compiler_params=pltpu.CompilerParams(collective_id=0, has_side_effects=True),
        name="gather_kv",
    )(keys, values, marks)


def compute_kernel(
    tile, lo_ref, q_ref, g_ref, rows_ref, span_ref, k_ref, v_ref, kp_ref, dq_ref, dk_ref, dv_ref, dk_acc, dv_acc
):
    i = pl.program_id(0)
    width = q_ref.shape[1]
    scaling = width ** (-0.5)

    @pl.when(i == 0)
    def _():
        dk_acc[...] = jnp.zeros_like(dk_acc)
        dv_acc[...] = jnp.zeros_like(dv_acc)

    q = q_ref[...]
    g = g_ref[...]
    lse = rows_ref[0:1, :]
    delta = rows_ref[1:2, :]
    start = span_ref[0:1, :]
    last = span_ref[1:2, :]
    dq_ref[...] = jnp.zeros_like(dq_ref)
    keys = STEPS * tile
    contract = (((1,), (1,)), ((), ()))

    def body(t, total):
        at = pl.ds(pl.multiple_of(t * tile, tile), tile)
        k = k_ref[:, at, :].reshape(keys, width)
        v = v_ref[:, at, :].reshape(keys, width)
        kp = kp_ref[:, at, :].reshape(keys, 1)
        s = lax.dot_general(k, q, contract, preferred_element_type=jnp.float32)
        ok = (kp <= last) & (kp >= start)
        p = jnp.where(ok, jnp.exp2(s * (scaling * LOG2E) - lse), 0.0)
        dp = lax.dot_general(v, g, contract, preferred_element_type=jnp.float32)
        ds = (p * (dp - delta)).astype(jnp.bfloat16)
        p = p.astype(jnp.bfloat16)
        dv = jnp.dot(p, g, preferred_element_type=jnp.float32)
        dk = jnp.dot(ds, q, preferred_element_type=jnp.float32)
        dv_acc[:, at, :] += dv.reshape(STEPS, tile, width)
        dk_acc[:, at, :] += dk.reshape(STEPS, tile, width)
        return total + lax.dot_general(
            ds, k, (((0,), (0,)), ((), ())), preferred_element_type=jnp.float32
        )

    total = lax.fori_loop(lo_ref[i], i + 1, body, jnp.zeros(q.shape, jnp.float32))
    dq_ref[...] = (total * scaling).astype(dq_ref.dtype)

    @pl.when(i == pl.num_programs(0) - 1)
    def _():
        dk_ref[...] = (dk_acc[...] * scaling).astype(dk_ref.dtype)
        dv_ref[...] = dv_acc[...].astype(dv_ref.dtype)


def compute(tile, lo, q, g, rows, span, kall, vall, kplaces):
    steps, tokens, width = kall.shape
    count = tokens // tile
    block = q.shape[0] // count
    part = jax.ShapeDtypeStruct(kall.shape, jnp.bfloat16)
    whole = lambda i, lo: (0, 0, 0)
    return pl.pallas_call(
        functools.partial(compute_kernel, tile),
        out_shape=(jax.ShapeDtypeStruct(q.shape, q.dtype), part, part),
        grid_spec=pltpu.PrefetchScalarGridSpec(
            num_scalar_prefetch=1,
            grid=(count,),
            in_specs=[
                pl.BlockSpec((block, width), lambda i, lo: (i, 0)),
                pl.BlockSpec((block, width), lambda i, lo: (i, 0)),
                pl.BlockSpec((2, block), lambda i, lo: (0, i)),
                pl.BlockSpec((2, block), lambda i, lo: (0, i)),
                pl.BlockSpec(kall.shape, whole),
                pl.BlockSpec(kall.shape, whole),
                pl.BlockSpec((steps, tokens, 1), whole),
            ],
            out_specs=[
                pl.BlockSpec((block, width), lambda i, lo: (i, 0)),
                pl.BlockSpec(kall.shape, whole),
                pl.BlockSpec(kall.shape, whole),
            ],
            scratch_shapes=[pltpu.VMEM(kall.shape, jnp.float32)] * 2,
        ),
        compiler_params=pltpu.CompilerParams(dimension_semantics=("arbitrary",)),
        name="block_grads",
    )(lo, q, g, rows, span, kall, vall, kplaces)


def reduce_kernel(
    n, pk, pv, ok, ov, near, both, far, mid, total, guest, send, recv
):
    b, h, even, partner, at = places(n)
    rows = pk.shape[1]
    size = rows // CHUNKS
    parts = (pk, pv)
    outs = (ok, ov)
    odd = jnp.logical_not(even)

    def copy(src, dst, kind, j, c, who):
        return pltpu.make_async_remote_copy(
            src_ref=src,
            dst_ref=dst,
            send_sem=send.at[kind, j, c],
            recv_sem=recv.at[kind, j, c],
            device_id=who,
            device_id_type=MESH,
        )

    greet(n)
    work = [(j, c, pl.ds(c * size, size)) for c in range(CHUNKS) for j in range(2)]
    give, own, skip, hop, side = {}, {}, {}, {}, {}
    gslot = jnp.where(even, 3, 1)
    for j, c, r in work:
        give[j, c] = copy(parts[j].at[gslot, r], near.at[j, r], 0, j, c, (partner, h))
        own[j, c] = copy(parts[j].at[1, r], both.at[j, r], 1, j, c, (partner, h))
        skip[j, c] = copy(parts[j].at[3, r], far.at[j, r], 2, j, c, (at(3), h))
        hop[j, c] = copy(mid.at[j, r], guest.at[0, j, r], 3, j, c, (at(2), h))
        side[j, c] = copy(total.at[j, r], guest.at[1, j, r], 4, j, c, (b, 1 - h))
        give[j, c].start()
    for j, c, r in work:
        give[j, c].wait_recv()
        mid[j, r] = (parts[j][2, r].astype(jnp.float32) + near[j, r].astype(jnp.float32)).astype(mid.dtype)
        hop[j, c].start()

        @pl.when(odd)
        def _():
            skip[j, c].start()

        @pl.when(even)
        def _():
            own[j, c].start()

    for j, c, r in work:
        hop[j, c].wait_recv()
        acc = parts[j][0, r].astype(jnp.float32) + guest[0, j, r].astype(jnp.float32)

        @pl.when(even)
        def _():
            skip[j, c].wait_recv()
            total[j, r] = (acc + far[j, r].astype(jnp.float32)).astype(total.dtype)

        @pl.when(odd)
        def _():
            own[j, c].wait_recv()
            total[j, r] = (acc + both[j, r].astype(jnp.float32)).astype(total.dtype)

        side[j, c].start()
    for j, c, r in work:
        side[j, c].wait_recv()
        outs[j][r] = (total[j, r].astype(jnp.float32) + guest[1, j, r].astype(jnp.float32)).astype(ok.dtype)
    for j, c, r in work:
        give[j, c].wait_send()
        hop[j, c].wait_send()
        side[j, c].wait_send()

        @pl.when(odd)
        def _():
            skip[j, c].wait_send()

        @pl.when(even)
        def _():
            own[j, c].wait_send()


def reduce_parts(n, pk, pv):
    steps, rows, width = pk.shape
    out = jax.ShapeDtypeStruct((rows, width), jnp.bfloat16)
    buf = pltpu.VMEM((2, rows, width), jnp.bfloat16)
    return pl.pallas_call(
        functools.partial(reduce_kernel, n),
        out_shape=(out, out),
        in_specs=[VMEM_SPEC] * 2,
        out_specs=(VMEM_SPEC, VMEM_SPEC),
        scratch_shapes=[
            buf,
            buf,
            buf,
            buf,
            buf,
            pltpu.VMEM((2, 2, rows, width), jnp.bfloat16),
            pltpu.SemaphoreType.DMA((5, 2, CHUNKS)),
            pltpu.SemaphoreType.DMA((5, 2, CHUNKS)),
        ],
        compiler_params=pltpu.CompilerParams(collective_id=1, has_side_effects=True),
        name="reduce_parts",
    )(pk, pv)


def on_device(
    n, queries, out_grad, outputs, key_vectors, value_vectors, logsumexp, positions, doc_start
):
    tokens, heads, width = queries.shape
    marks = jnp.broadcast_to(positions[:1], (8, width))
    kall, vall, marks = gather(n, key_vectors, value_vectors, marks)
    row_delta = jnp.sum(out_grad.astype(jnp.float32) * outputs.astype(jnp.float32), axis=-1)
    rows = jnp.stack([(logsumexp * LOG2E).reshape(-1), row_delta.reshape(-1)])
    span = jnp.stack([jnp.repeat(doc_start, heads), jnp.repeat(positions, heads)])
    kplaces = (jnp.arange(tokens, dtype=jnp.int32)[None, :] * n + marks[:, 0, :1])[:, :, None]
    lo = doc_start[::TILE] // n // TILE
    dq, pk, pv = compute(
        TILE,
        lo,
        queries.reshape(-1, width),
        out_grad.reshape(-1, width),
        rows,
        span,
        kall,
        vall,
        kplaces,
    )
    dk, dv = reduce_parts(n, pk, pv)
    return dq.reshape(queries.shape), dk, dv


def solution(mesh):
    n = mesh.shape["blk"]
    in_specs = (
        P("blk", "head", None),
        P("blk", "head", None),
        P("blk", "head", None),
        P("blk", None),
        P("blk", None),
        P("blk", "head"),
        P("blk"),
        P("blk"),
    )
    out_specs = (P("blk", "head", None), P("blk", None), P("blk", None))
    return jax.shard_map(
        functools.partial(on_device, n),
        mesh=mesh,
        in_specs=in_specs,
        out_specs=out_specs,
        check_vma=False,
    )
```

time: 120 us -> 68.1 us (0.57)
  matrix products: 59.4 us -> 0 us
  Pallas kernels: 0 us -> 52.6 us
  starting transfers between devices: 26.4 us -> 0 us
  blocking collectives: 19.1 us -> 0 us
  waiting for transfers between devices: 8.36 us -> 0 us
  local copies, waits for them, and re-layouts: 2.48 us -> 8.27 us
  other arithmetic: 2.42 us -> 5.83 us
    dot_general x20 -> x0, matrix products: 59.4 us -> none  [the longest x4 18.5 us: block_grads(): jnp.einsum('thd,kd->htk', out_grad, value_vectors, preferred_element_type...]
    pallas_call x0 -> x3, Pallas kernels: none -> 52.6 us  [the longest x1 21.3 us: reduce_parts(): pl.pallas_call(functools.partial(reduce_kernel, n), out_shape=(out, out),...]
    ppermute x17 -> x0, starting transfers between devices: 26.4 us -> none  [from_behind(): return lax.ppermute(block, axis, route)]
    psum x1 -> x0, blocking collectives: 19.1 us -> none  [on_device(): key_total, value_total = lax.psum((key_total, value_total), 'head')]
    ppermute x17 -> x0, waiting for transfers between devices: 8.36 us -> none  [from_behind(): return lax.ppermute(block, axis, route)]
    slice x0 -> x3, local copies, waits for them, and re-layouts: none -> 2.84 us  [the longest x1 1.19 us: on_device(): marks = jnp.broadcast_to(positions[:1], (8, width))]
    reduce_sum x1, other arithmetic: 0.64 us -> 2.17 us  [on_device(): jnp.sum(out_grad.astype(jnp.float32) * outputs.astype(jnp.float32), axis=-1)]
    broadcast_in_dim x0 -> x3, local copies, waits for them, and re-layouts: none -> 1.48 us  [the longest x1 1.24 us: on_device(): marks = jnp.broadcast_to(positions[:1], (8, width))]
  transfers between devices with their start and end apart: 17 -> 0, of which waited for: 4 -> 0; matrix products, arithmetic and copies ran while one was open for 53% -> 0% of each run, Pallas kernels for 0% -> 0%
where the time goes in v1:
time: 68.1 us; the launch traced here: 67.4 us
  Pallas kernels  52.6 us (77%)
  local copies, waits for them, and re-layouts  8.27 us (12%)
  other arithmetic  5.83 us (9%)
  between operations  0.74 us (1%)
    pallas_call x1, Pallas kernels, reduce_parts(): pl.pallas_call(functools.partial(reduce_kernel, n), out_shape=(out, out),...  21.3 us
    pallas_call x1, Pallas kernels, gather(): pl.pallas_call(functools.partial(gather_kernel, n), out_shape=(shape, sha...  17.3 us
    pallas_call x1, Pallas kernels, compute(): pl.pallas_call(functools.partial(compute_kernel, tile), out_shape=(jax.Sh...  13.9 us
    unnamed x6, local copies, waits for them, and re-layouts  3.15 us
    reduce_sum x1, other arithmetic, on_device(): jnp.sum(out_grad.astype(jnp.float32) * outputs.astype(jnp.float32), axis=-1)  2.17 us

profile of v1, /device:TPU:1, one launch (start us, length us, event | category | flops | bytes accessed | tf_op | source)
XLA Modules:
  0.0 67.4 jit_solution(8316042872747588525)
XLA Ops:
  0.6 1.2 %slice.12 = s32[1]{0:T(128)} slice(s32[512]{0:T(512)} %param.14), slice={[0:1]} | slice | bytes 8 | tf_op jit(solution)/shard_map/slice | solution.py:338
  1.8 0.8 %slice.11 = s32[8]{0:T(128)S(1)} slice(s32[512]{0:T(512)} %param.15), slice={[0:512:64]} | slice | bytes 64 | tf_op jit(solution)/shard_map/slice | solution.py:344
  2.6 0.5 and_select_fusion.lo_ref
  3.1 1.2 %broadcast_in_dim.15.pos_ref = s32[8,128]{1,0:T(8,128)} broadcast(s32[]{:T(128)} %bitcast.2), dimensions={} | broadcast | bytes 4100 | tf_op jit(solution)/shard_map/broadcast_in_dim | solution.py:338
  4.3 0.7 %broadcast_multiply_fusion = f32[512,8]{0,1:T(8,128)S(1)} fusion(f32[512,8]{0,1:T(8,128)} %param.13), kind=kLoop, calls=%fused_computation.4 | loop fusion | flops 4096 | bytes 32768 | tf_op jit(solution)/shard_map/mul | solution.py:341
  5.1 0.1 copy.12
  5.2 0.2 stack_reshape.12
  5.4 0.0 copy-start
  5.4 0.0 copy-start.1
  5.4 2.2 %multiply_reduce_fusion = f32[512,8]{1,0:T(8,128)S(1)} fusion(bf16[512,8,128]{2,1,0:T(8,128)(2,1)} %param.10, bf16[512,8,128]{2,1,0:T(8,128)(2,1)} %param.9), kind=kLoop, calls=%fused_computation | loop fusion | flops 2093056 | bytes 2113536 | tf_op jit(solution)/shard_map/reduce_sum | solution.py:340
  7.6 0.2 stack_reshape.13
  7.7 0.6 pad_maximum_fusion.rows_ref
  8.4 0.0 copy-done
  8.4 0.1 broadcast_in_dim.14
  8.5 0.2 stack_reshape.15
  8.7 0.0 copy-done.1
  8.7 0.1 broadcast_in_dim.6
  8.8 0.2 stack_reshape.14
  9.0 0.6 pad_add_fusion.span_ref
  9.7 17.3 %gather_kv.1 = (bf16[4,512,128]{2,1,0:T(8,128)(2,1)}, bf16[4,512,128]{2,1,0:T(8,128)(2,1)}, s32[4,8,128]{2,1,0:T(8,128)}) custom-call(bf16[512,128]{1,0:T(8,128)(2,1)} %k_ref.1, bf16[512,128]{1,0:T(8,128)(2,1)} %v_ref.1, s32[8,128]{1,0:T(8,128)} %broadcast_in_dim.15.pos_ref), custom_call_target="tpu_custom_call" | custom-call | tf_op jit(solution)/shard_map/gather_kv/pallas_call | solution.py:136
  27.0 0.9 %slice_reduce_fusion = s32[4]{0:T(128)S(1)} fusion(s32[4,8,128]{2,1,0:T(8,128)} %get-tuple-element.13), kind=kLoop, calls=%fused_computation.5 | loop fusion | bytes 32 | tf_op jit(solution)/shard_map/slice | solution.py:343
  27.9 1.1 %broadcast_add_fusion.kp_ref = s32[4,512,1]{2,1,0:T(8,128)} fusion(s32[4]{0:T(128)S(1)} %slice_reduce_fusion, s32[512]{0:T(512)S(1)} %iota_multiply_fusion), kind=kLoop, calls=%fused_computation.1 | loop fusion | flops 2048 | bytes 10256 | tf_op jit(solution)/shard_map/add | solution.py:343
  29.0 13.9 %block_grads.1 = (bf16[4096,128]{1,0:T(8,128)(2,1)}, bf16[4,512,128]{2,1,0:T(8,128)(2,1)}, bf16[4,512,128]{2,1,0:T(8,128)(2,1)}) custom-call(s32[8]{0:T(128)} %and_select_fusion.lo_ref, bf16[4096,128]{1,0:T(8,128)(2,1)} %bitcast.5, bf16[4096,128]{1,0:T(8,128)(2,1)} %bitcast.4, f32[2,4096]{1,0:T(2,128)} %pad_maximum_fusion.rows_ref, ...), custom_call_target="tpu_custom_call" | custom-call | tf_op jit(solution)/shard_map/block_grads/pallas_call | solution.py:207
  43.0 21.3 %reduce_parts.1 = (bf16[512,128]{1,0:T(8,128)(2,1)}, bf16[512,128]{1,0:T(8,128)(2,1)}) custom-call(bf16[4,512,128]{2,1,0:T(8,128)(2,1)} %get-tuple-element.15.pk, bf16[4,512,128]{2,1,0:T(8,128)(2,1)} %get-tuple-element.16.pv), custom_call_target="tpu_custom_call" | custom-call | tf_op jit(solution)/shard_map/reduce_parts/pallas_call | solution.py:314
  64.3 1.6 %copy.15 = bf16[512,128]{1,0:T(8,128)(2,1)} copy(bf16[512,128]{1,0:T(8,128)(2,1)} %get-tuple-element.23) | data formatting | bytes 262144
  65.8 1.6 %copy.16 = bf16[512,128]{1,0:T(8,128)(2,1)} copy(bf16[512,128]{1,0:T(8,128)(2,1)} %get-tuple-element.24) | data formatting | bytes 262144
  (1 shorter events, 0.0 us)
Async XLA Ops:
  5.4 3.0 %copy-start = (s32[512]{0:T(512)S(1)}, s32[512]{0:T(512)}, u32[]{:S(2)}) copy-start(s32[512]{0:T(512)} %param.14) | copy-start | bytes 6148
  5.4 3.3 %copy-start.1 = (s32[512]{0:T(512)S(1)}, s32[512]{0:T(512)}, u32[]{:S(2)}) copy-start(s32[512]{0:T(512)} %param.15) | copy-start | bytes 6148
